TPU v7x, 256 devices: a whole 4x4x8 slice. The times are simulated.
256 devices in a mesh: sa: 32 (over z_lo, x, core), sb: 8 (over z_hi, y).
Axes of the slice: x: 4, y: 4, z: 8 (z_hi: 2, z_lo: 4; z = z_hi * 4 + z_lo), core: 2. Of those that a mesh axis runs over, the one named last changes fastest.
Arguments:
- tokens: bfloat16 [64, 32, 32, 2048], P('sa', 'sb'), may hold values from -6 to 6
- norm_gain: float32 [2048], replicated, may hold values from 0.5 to 1.5
- gate_weight: bfloat16 [2048, 2048], P(('sa', 'sb')), may hold values from -0.125 to 0.125
- level_one: bfloat16 [32, 32, 64, 64], P('sb', 'sa'), may hold values from -0.75 to 0.75
- level_two: bfloat16 [64, 32, 32, 32], P('sa', 'sb'), may hold values from -1 to 1
- level_three: bfloat16 [64, 32, 32, 32], P('sa', 'sb'), may hold values from -1 to 1
- upstream: bfloat16 [64, 32, 32, 2048], P('sa', 'sb'), may hold values from -6 to 6
Outputs:
- output: bfloat16 [64, 32, 32, 2048], P('sa', 'sb')
- grad_tokens: bfloat16 [64, 32, 32, 2048], P('sa', 'sb')
- grad_one: float32 [32, 32, 64, 64], P('sb', 'sa')
- grad_two: float32 [64, 32, 32, 32], P('sa', 'sb')
- grad_three: float32 [64, 32, 32, 32], P('sa', 'sb')
All inputs are finite; a program needn't handle non-finite values.
Results may differ from a plain program's by a relative error of at most 0.0071.
Values may be sent and summed in bfloat16 or wider, within the bound.
A program may use at most 128 MiB of HBM per device.

v0:
```python
import jax
import jax.numpy as jnp
from jax import lax
from jax.sharding import PartitionSpec as P

ALL = ("sa", "sb")
EPSILON = 1e-06


def to_blocks(values):
    i, j, k, c = values.shape
    sa, sb = (lax.axis_size("sa"), lax.axis_size("sb"))
    parts = values.reshape(i, j, sa, sb, c // sb).transpose(2, 3, 0, 1, 4)
    parts = parts.reshape(sa * sb, i * j, c // sb)
    parts = lax.all_to_all(parts, ALL, split_axis=0, concat_axis=0, tiled=True)
    parts = parts.reshape(sa, sb, i, j, c // sb).transpose(0, 2, 1, 3, 4)
    return parts.reshape(sa * i, sb * j, c // sb)


def from_blocks(values):
    sa, sb = (lax.axis_size("sa"), lax.axis_size("sb"))
    i, j, c = (values.shape[0] // sa, values.shape[1] // sb, values.shape[2])
    parts = values.reshape(sa, i, sb, j, c).transpose(0, 2, 1, 3, 4)
    parts = parts.reshape(sa * sb, i * j, c)
    parts = lax.all_to_all(parts, ALL, split_axis=0, concat_axis=0, tiled=True)
    parts = parts.reshape(sa, sb, i, j, c).transpose(2, 3, 0, 1, 4)
    return parts.reshape(i, j, sa, sb * c)


def dot(pattern, left, right):
    return jnp.einsum(pattern, left, right, preferred_element_type=jnp.float32)


def body(tokens, norm_gain, gate_weight, level_one, level_two, level_three, upstream):
    channels = tokens.shape[3]
    sa, sb = (lax.axis_size("sa"), lax.axis_size("sb"))
    grad_scale = channels ** (-0.5)
    gathered = lax.all_gather(gate_weight, ALL, axis=0, tiled=True)
    block_one = lax.all_gather(level_one[:, 0], "sb", axis=0, tiled=True)
    block_two = lax.all_gather(level_two, "sb", axis=1, tiled=True)
    block_two = lax.all_to_all(block_two, "sa", split_axis=1, concat_axis=0, tiled=True)[:, 0]
    tokens_float = tokens.astype(jnp.float32)
    inverse_rms = lax.rsqrt(jnp.mean(tokens_float * tokens_float, axis=3, keepdims=True) + EPSILON)
    normed = (tokens_float * inverse_rms * norm_gain).astype(jnp.bfloat16)
    normed_block = to_blocks(normed)
    first_mix = dot("joi,ijc->ojc", block_one, normed_block).astype(jnp.bfloat16)
    second_mix = dot("ioj,ijc->ioc", block_two, first_mix).astype(jnp.bfloat16)
    second_mix = from_blocks(second_mix)
    mixed_all = dot("ijok,ijkc->ijoc", level_three, second_mix)
    token_rows = normed.reshape(-1, channels)
    gate_pre = dot("tr,rc->tc", token_rows, gathered).reshape(tokens.shape)
    gate_sigmoid = jax.nn.sigmoid(gate_pre)
    gate_value = gate_pre * gate_sigmoid
    output = (tokens_float + mixed_all * gate_value).astype(jnp.bfloat16)
    upstream_float = upstream.astype(jnp.float32)
    grad_mixed = (upstream_float * gate_value).astype(jnp.bfloat16)
    grad_gate = (
        upstream_float * mixed_all * gate_sigmoid * (1.0 + gate_pre * (1.0 - gate_sigmoid))
    ).astype(jnp.bfloat16)
    grad_second = dot("ijok,ijoc->ijkc", level_three, grad_mixed).astype(jnp.bfloat16)
    grad_block = to_blocks(grad_second)
    grad_first = dot("ioj,ioc->ijc", block_two, grad_block).astype(jnp.bfloat16)
    grad_normed = dot("joi,ojc->ijc", block_one, grad_first).astype(jnp.bfloat16)
    grad_normed = from_blocks(grad_normed)
    grad_three = dot("ijoc,ijkc->ijok", grad_mixed, second_mix) * grad_scale
    part_two = dot("ioc,ijc->ioj", grad_block, first_mix).astype(jnp.bfloat16)
    part_one = dot("ojc,ijc->joi", grad_first, normed_block).astype(jnp.bfloat16)
    part_two = lax.all_to_all(part_two[:, None], "sa", split_axis=0, concat_axis=1, tiled=True)
    m1, m2 = (part_one.shape[1], part_two.shape[2])
    own_i, own_k = (part_two.shape[0], part_two.shape[1] // sb)
    own_j = part_one.shape[0] // sb
    packed = jnp.concatenate(
        [
            part_one.reshape(sb, -1),
            part_two.reshape(own_i, sb, own_k, m2, m2).transpose(1, 0, 2, 3, 4).reshape(sb, -1),
        ],
        axis=1,
    )
    packed = lax.all_to_all(packed, "sb", split_axis=0, concat_axis=0, tiled=True)
    summed = jnp.sum(packed.astype(jnp.float32), axis=0) * grad_scale
    cut = own_j * m1 * m1
    grad_one = summed[:cut].reshape(own_j, 1, m1, m1)
    grad_two = summed[cut:].reshape(own_i, own_k, m2, m2)
    back_term = dot("tc,rc->tr", grad_gate.reshape(-1, channels), gathered)
    grad_hidden = grad_normed.astype(jnp.float32) + back_term.reshape(tokens.shape)
    weighted = grad_hidden * norm_gain
    average = jnp.mean(weighted * tokens_float, axis=3, keepdims=True)
    grad_tokens = (
        upstream_float + inverse_rms * weighted - tokens_float * inverse_rms**3 * average
    ).astype(jnp.bfloat16)
    return (output, grad_tokens, grad_one, grad_two, grad_three)


def solution(mesh):
    token_spec = P("sa", "sb", None, None)
    block_spec = P("sb", "sa", None, None)
    in_specs = (token_spec, P(), P(ALL, None), block_spec, token_spec, token_spec, token_spec)
    out_specs = (token_spec, token_spec, block_spec, token_spec, token_spec)
    return jax.shard_map(body, mesh=mesh, in_specs=in_specs, out_specs=out_specs, check_vma=False)
```

profile of v0, /device:TPU:1, one launch (start us, length us, event | category | flops | bytes accessed | tf_op | source)
XLA Modules:
  0.0 908.0 jit_solution(1630995716396295364)
XLA Ops:
  8.8 42.1 %all_gather.10 = bf16[2,32,32,32]{3,2,0,1:T(8,128)(2,1)S(1)} all-gather(bf16[2,4,32,32]{3,2,0,1:T(8,128)(2,1)S(1)} %copy.129), channel_id=1, replica_groups=mesh['sa'=32,'sb'=8] {'sb'}, dimensions={1}, use_global_device_ids=true | all-gather | bytes 147456 | tf_op jit(solution)/shard_map/all_gather | solution.py:40
  52.0 12.8 %all-to-all-start.1 = ((bf16[32,2,1024]{2,1,0:T(2,128)(2,1)}), bf16[32,2,1024]{2,1,0:T(2,128)(2,1)S(1)}, u32[]{:S(2)}, u32[]{:S(2)}) async-start(bf16[32,2,1024]{2,1,0:T(2,128)(2,1)} %reshape.141), calls=%async_computation.1 | async-start | bytes 262144 | tf_op jit(solution)/shard_map/all_to_all | solution.py:41
  67.3 6.0 all-to-all-done.1
  73.3 9.9 %all-to-all-start = ((bf16[256,8,256]{2,1,0:T(8,128)(2,1)}), bf16[256,8,256]{2,1,0:T(8,128)(2,1)S(1)}, u32[]{:S(2)}, u32[]{:S(2)}) async-start(bf16[256,8,256]{2,1,0:T(8,128)(2,1)} %copy.154), calls=%async_computation | async-start | bytes 2097152 | tf_op jit(solution)/shard_map/all_to_all | solution.py:15
  83.2 60.6 %all-gather = bf16[32,1,64,64]{3,2,1,0:T(8,128)(2,1)S(1)} all-gather(bf16[4,1,64,64]{3,2,1,0:T(8,128)(2,1)S(1)} %copy-done.11), channel_id=2, replica_groups=mesh['sa'=32,'sb'=8] {'sb'}, dimensions={0}, use_global_device_ids=true | all-gather | bytes 294912 | tf_op jit(solution)/shard_map/all_gather | solution.py:39
  150.1 42.8 %all_to_all.59 = bf16[256,8,256]{2,1,0:T(8,128)(2,1)S(1)} all-to-all(bf16[256,8,256]{2,1,0:T(8,128)(2,1)S(1)} %copy.132), channel_id=1, replica_groups=mesh['sa'=32,'sb'=8] {'sa','sb'}, dimensions={0} | all-to-all | bytes 2097152 | tf_op jit(solution)/shard_map/all_to_all | solution.py:25
  195.6 1.8 convolution_bitcast_fusion
  197.4 546.0 %all-gather.3.cloned.1.call-done = bf16[2048,2048]{1,0:T(8,128)(2,1)} async-done(((bf16[8,2048]{1,0:T(8,128)(2,1)}), bf16[2048,2048]{1,0:T(8,128)(2,1)}) %all-gather.3.cloned.1.call-update) | async-done | bytes 8388624 | tf_op jit(solution)/shard_map/all_gather | solution.py:38
  743.4 9.3 %fusion.10 = (bf16[2,4,32,2048]{3,2,1,0:T(8,128)(2,1)S(1)}, bf16[2,4,32,2048]{3,2,1,0:T(8,128)(2,1)}, f32[2,4,32,2048]{3,2,1,0:T(8,128)}) fusion(bf16[2,4,32,2048]{3,2,1,0:T(8,128)(2,1)} %param.13, f32[2,4,32,2048]{3,2,1,0:T(8,128)} %convolution_bitcast_fusion, bf16[2,4,32,2048]{3,2,1,0:T(8,128)(2,1)} %param.7, ...), kind=kOutput, calls=%fused_computation.16 | convolution fusion | flops 2155347968 | bytes 16786432 | tf_op jit(solution)/shard_map/tr,rc->tc/dot_general | solution.py:31
  754.4 44.5 %all_to_all.60 = bf16[256,8,256]{2,1,0:T(8,128)(2,1)S(1)} all-to-all(bf16[256,8,256]{2,1,0:T(8,128)(2,1)S(1)} %copy.156), channel_id=1, replica_groups=mesh['sa'=32,'sb'=8] {'sa','sb'}, dimensions={0} | all-to-all | bytes 2097152 | tf_op jit(solution)/shard_map/all_to_all | solution.py:15
  799.1 2.3 copy.137
  801.4 2.1 reshape.131
  803.5 2.9 fusion.27
  806.9 2.2 reshape.143
  809.2 5.9 all-to-all-start.5
  818.1 5.6 all-to-all-done.5
  829.3 2.0 reshape.145
  831.3 4.1 all-to-all-start.6
  835.4 1.9 fusion.24
  841.0 6.0 all-to-all-done.6
  846.9 10.8 %all-to-all-start.4 = ((bf16[256,8,256]{2,1,0:T(8,128)(2,1)}), bf16[256,8,256]{2,1,0:T(8,128)(2,1)}, u32[]{:S(2)}, u32[]{:S(2)}) async-start(bf16[256,8,256]{2,1,0:T(8,128)(2,1)} %copy.142), calls=%async_computation.4 | async-start | bytes 2097152 | tf_op jit(solution)/shard_map/all_to_all | solution.py:25
  858.8 2.6 reshape.146
  863.9 24.2 %all-to-all-done.4 = bf16[256,8,256]{2,1,0:T(8,128)(2,1)} async-done(((bf16[256,8,256]{2,1,0:T(8,128)(2,1)}), bf16[256,8,256]{2,1,0:T(8,128)(2,1)}, u32[]{:S(2)}, u32[]{:S(2)}) %all-to-all-start.4) | async-done | bytes 1048608 | tf_op jit(solution)/shard_map/all_to_all | solution.py:25
  891.1 8.4 fusion.21
  (74 shorter events, 36.7 us)
Async XLA Ops:
  7.2 188.4 %copy-start = (bf16[2,4,32,32]{3,2,1,0:T(8,128)(2,1)S(1)}, bf16[2,4,32,32]{3,2,1,0:T(8,128)(2,1)}, u32[]{:S(2)}) copy-start(bf16[2,4,32,32]{3,2,1,0:T(8,128)(2,1)} %param.12) | copy-start | bytes 49156
  7.2 57.6 %copy-start.2 = (bf16[2,4,32,2048]{3,2,1,0:T(8,128)(2,1)S(1)}, bf16[2,4,32,2048]{3,2,1,0:T(8,128)(2,1)}, u32[]{:S(2)}) copy-start(bf16[2,4,32,2048]{3,2,1,0:T(8,128)(2,1)} %param.7) | copy-start | bytes 3145732
  7.2 57.9 %copy-start.12 = (f32[2048]{0:T(1024)S(1)}, f32[2048]{0:T(1024)}, u32[]{:S(2)}) copy-start(f32[2048]{0:T(1024)} %param.8) | copy-start | bytes 24580
  7.2 736.2 %all-gather.3.cloned.1.call-start = ((), (), s32[]{:S(2)}) async-start(), calls=%async_computation.7 | async-start | bytes 8421376 | tf_op jit(solution)/shard_map/all_gather | solution.py:38
  52.0 21.3 %all-to-all-start.1 = ((bf16[32,2,1024]{2,1,0:T(2,128)(2,1)}), bf16[32,2,1024]{2,1,0:T(2,128)(2,1)S(1)}, u32[]{:S(2)}, u32[]{:S(2)}) async-start(bf16[32,2,1024]{2,1,0:T(2,128)(2,1)} %reshape.141), calls=%async_computation.1 | async-start | bytes 262144 | tf_op jit(solution)/shard_map/all_to_all | solution.py:41
  65.7 17.5 %copy-start.11 = (bf16[4,1,64,64]{3,2,1,0:T(8,128)(2,1)S(1)}, bf16[4,1,64,64]{3,2,1,0:T(8,128)(2,1)}, u32[]{:S(2)}) copy-start(bf16[4,1,64,64]{3,2,1,0:T(8,128)(2,1)} %param.10) | copy-start | bytes 98308
  73.3 70.8 %all-to-all-start = ((bf16[256,8,256]{2,1,0:T(8,128)(2,1)}), bf16[256,8,256]{2,1,0:T(8,128)(2,1)S(1)}, u32[]{:S(2)}, u32[]{:S(2)}) async-start(bf16[256,8,256]{2,1,0:T(8,128)(2,1)} %copy.154), calls=%async_computation | async-start | bytes 2097152 | tf_op jit(solution)/shard_map/all_to_all | solution.py:15
  143.8 2.0 copy-start.6
  144.1 2.2 copy-start.4
  752.7 1.0 copy-start.8
  803.5 2.9 copy-start.1
  803.5 2.9 copy-start.5
  809.2 14.6 %all-to-all-start.5 = ((bf16[32,2,1024]{2,1,0:T(2,128)(2,1)}), bf16[32,2,1024]{2,1,0:T(2,128)(2,1)}, u32[]{:S(2)}, u32[]{:S(2)}) async-start(bf16[32,2,1024]{2,1,0:T(2,128)(2,1)} %reshape.143), calls=%async_computation.5 | async-start | bytes 262144 | tf_op jit(solution)/shard_map/all_to_all | solution.py:68
  825.0 10.4 %copy-start.7 = (bf16[32,1,64,64]{3,2,1,0:T(8,128)(2,1)S(1)}, bf16[32,1,64,64]{3,2,1,0:T(8,128)(2,1)}, u32[]{:S(2)}) copy-start(bf16[32,1,64,64]{3,2,1,0:T(8,128)(2,1)} %copy-done.6) | copy-start | bytes 786436
  831.3 15.6 %all-to-all-start.6 = ((bf16[8,2,12288]{2,1,0:T(2,128)(2,1)}), bf16[8,2,12288]{2,1,0:T(2,128)(2,1)}, u32[]{:S(2)}, u32[]{:S(2)}) async-start(bf16[8,2,12288]{2,1,0:T(2,128)(2,1)} %reshape.145), calls=%async_computation.6 | async-start | bytes 786432 | tf_op jit(solution)/shard_map/all_to_all | solution.py:79
  839.4 18.3 %copy-start.9 = (bf16[2,4,32,2048]{3,2,1,0:T(8,128)(2,1)S(1)}, bf16[2,4,32,2048]{3,2,1,0:T(8,128)(2,1)}, u32[]{:S(2)}) copy-start(bf16[2,4,32,2048]{3,2,1,0:T(8,128)(2,1)} %copy-done.8) | copy-start | bytes 3145732
  846.9 41.2 %all-to-all-start.4 = ((bf16[256,8,256]{2,1,0:T(8,128)(2,1)}), bf16[256,8,256]{2,1,0:T(8,128)(2,1)}, u32[]{:S(2)}, u32[]{:S(2)}) async-start(bf16[256,8,256]{2,1,0:T(8,128)(2,1)} %copy.142), calls=%async_computation.4 | async-start | bytes 2097152 | tf_op jit(solution)/shard_map/all_to_all | solution.py:25
  889.6 1.5 copy-start.3
  891.1 8.4 copy-start.10
Sparse Core Ops, SparseCore 0:
  9.9 733.4 all-gather.2
where the time goes:
time: 909 us; the launch traced here: 908 us
  waiting for transfers between devices  588 us (65%)
  blocking collectives  190 us (21%)
  starting transfers between devices  43.5 us (5%)
  local copies, waits for them, and re-layouts  35.9 us (4%)
  matrix products  30.1 us (3%)
  between operations  14.4 us (2%)
    all_gather x1, waiting for transfers between devices, body(): gathered = lax.all_gather(gate_weight, ALL, axis=0, tiled=True)  546 us
    all_gather x1, blocking collectives, body(): block_one = lax.all_gather(level_one[:, 0], 'sb', axis=0, tiled=True)  60.6 us
    all_to_all x1, blocking collectives, to_blocks(): parts = lax.all_to_all(parts, ALL, split_axis=0, concat_axis=0, tiled=True)  44.5 us
    all_to_all x1, blocking collectives, from_blocks(): parts = lax.all_to_all(parts, ALL, split_axis=0, concat_axis=0, tiled=True)  42.8 us
    all_gather x1, blocking collectives, body(): block_two = lax.all_gather(level_two, 'sb', axis=1, tiled=True)  42.1 us
    dot_general x11, matrix products, dot(): return jnp.einsum(pattern, left, right, preferred_element_type=jnp.float32)  30.1 us
    all_to_all x1, waiting for transfers between devices, from_blocks(): parts = lax.all_to_all(parts, ALL, split_axis=0, concat_axis=0, tiled=True)  24.2 us
  transfers between devices with their start and end apart: 6, of which 5 were waited for; matrix products, arithmetic and copies ran while one was open for 3% of the time, Pallas kernels for 0%

commit v1 on v0

--- a/solution.py
+++ b/solution.py
@@ -35,7 +35,10 @@
     channels = tokens.shape[3]
     sa, sb = (lax.axis_size("sa"), lax.axis_size("sb"))
     grad_scale = channels ** (-0.5)
-    gathered = lax.all_gather(gate_weight, ALL, axis=0, tiled=True)
+    n_dev = lax.axis_size(ALL)
+    blocks = jnp.stack([gate_weight for _ in range(n_dev)])
+    blocks = lax.all_to_all(blocks, ALL, split_axis=0, concat_axis=0)
+    gathered = jnp.concatenate(blocks, axis=0)
     block_one = lax.all_gather(level_one[:, 0], "sb", axis=0, tiled=True)
     block_two = lax.all_gather(level_two, "sb", axis=1, tiled=True)
     block_two = lax.all_to_all(block_two, "sa", split_axis=1, concat_axis=0, tiled=True)[:, 0]

time: 909 us -> 538 us (0.59)
  waiting for transfers between devices: 588 us -> 225 us
  between operations: 14.4 us -> 1.06 us
    all_gather x1 -> x0, waiting for transfers between devices: 546 us -> none  [body(): gathered = lax.all_gather(gate_weight, ALL, axis=0, tiled=True)]
    all_to_all x0 -> x1, waiting for transfers between devices: none -> 183 us  [body(): blocks = lax.all_to_all(blocks, ALL, split_axis=0, concat_axis=0)]
  transfers between devices with their start and end apart: 6 -> 6, of which waited for: 5 -> 5; matrix products, arithmetic and copies ran while one was open for 3% -> 4% of each run, Pallas kernels for 0% -> 0%
where the time goes in v1:
time: 538 us; the launch traced here: 537 us
  waiting for transfers between devices  225 us (42%)
  blocking collectives  183 us (34%)
  starting transfers between devices  52 us (10%)
  local copies, waits for them, and re-layouts  40.3 us (7%)
  matrix products  30.1 us (6%)
  other arithmetic  5.7 us (1%)
    all_to_all x1, waiting for transfers between devices, body(): blocks = lax.all_to_all(blocks, ALL, split_axis=0, concat_axis=0)  183 us
    all_gather x1, blocking collectives, body(): block_one = lax.all_gather(level_one[:, 0], 'sb', axis=0, tiled=True)  60.1 us
    all_to_all x1, blocking collectives, from_blocks(): parts = lax.all_to_all(parts, ALL, split_axis=0, concat_axis=0, tiled=True)  43.2 us
    all_gather x1, blocking collectives, body(): block_two = lax.all_gather(level_two, 'sb', axis=1, tiled=True)  41.9 us
    all_to_all x1, blocking collectives, to_blocks(): parts = lax.all_to_all(parts, ALL, split_axis=0, concat_axis=0, tiled=True)  37.4 us
    dot_general x11, matrix products, dot(): return jnp.einsum(pattern, left, right, preferred_element_type=jnp.float32)  30.1 us
    all_to_all x1, waiting for transfers between devices, from_blocks(): parts = lax.all_to_all(parts, ALL, split_axis=0, concat_axis=0, tiled=True)  24.2 us
    all_to_all x1, starting transfers between devices, body(): lax.all_to_all(block_two, 'sa', split_axis=1, concat_axis=0, tiled=True)  12.9 us
  transfers between devices with their start and end apart: 6, of which 5 were waited for; matrix products, arithmetic and copies ran while one was open for 4% of the time, Pallas kernels for 0%

profile of v1, /device:TPU:1, one launch (start us, length us, event | category | flops | bytes accessed | tf_op | source)
XLA Modules:
  0.0 536.7 jit_solution(1056388482337025485)
XLA Ops:
  1.6 41.9 %all_gather.7 = bf16[2,32,32,32]{3,2,0,1:T(8,128)(2,1)S(1)} all-gather(bf16[2,4,32,32]{3,2,0,1:T(8,128)(2,1)S(1)} %copy.129), channel_id=1, replica_groups=mesh['sa'=32,'sb'=8] {'sb'}, dimensions={1}, use_global_device_ids=true | all-gather | bytes 147456 | tf_op jit(solution)/shard_map/all_gather | solution.py:43
  44.7 12.9 %all-to-all-start.1 = ((bf16[32,2,1024]{2,1,0:T(2,128)(2,1)}), bf16[32,2,1024]{2,1,0:T(2,128)(2,1)S(1)}, u32[]{:S(2)}, u32[]{:S(2)}) async-start(bf16[32,2,1024]{2,1,0:T(2,128)(2,1)} %reshape.147), calls=%async_computation.1 | async-start | bytes 262144 | tf_op jit(solution)/shard_map/all_to_all | solution.py:44
  60.1 6.0 %all-to-all-done.1 = bf16[32,2,1024]{2,1,0:T(2,128)(2,1)S(1)} async-done(((bf16[32,2,1024]{2,1,0:T(2,128)(2,1)}), bf16[32,2,1024]{2,1,0:T(2,128)(2,1)S(1)}, u32[]{:S(2)}, u32[]{:S(2)}) %all-to-all-start.1) | async-done | bytes 131104 | tf_op jit(solution)/shard_map/all_to_all | solution.py:44
  66.1 9.9 %all-to-all-start = ((bf16[256,8,256]{2,1,0:T(8,128)(2,1)}), bf16[256,8,256]{2,1,0:T(8,128)(2,1)S(1)}, u32[]{:S(2)}, u32[]{:S(2)}) async-start(bf16[256,8,256]{2,1,0:T(8,128)(2,1)} %copy.154), calls=%async_computation | async-start | bytes 2097152 | tf_op jit(solution)/shard_map/all_to_all | solution.py:15
  76.0 60.1 %all-gather = bf16[32,1,64,64]{3,2,1,0:T(8,128)(2,1)S(1)} all-gather(bf16[4,1,64,64]{3,2,1,0:T(8,128)(2,1)S(1)} %copy-done.12), channel_id=2, replica_groups=mesh['sa'=32,'sb'=8] {'sb'}, dimensions={0}, use_global_device_ids=true | all-gather | bytes 294912 | tf_op jit(solution)/shard_map/all_gather | solution.py:42
  142.5 43.2 %all_to_all.64 = bf16[256,8,256]{2,1,0:T(8,128)(2,1)S(1)} all-to-all(bf16[256,8,256]{2,1,0:T(8,128)(2,1)S(1)} %copy.132), channel_id=1, replica_groups=mesh['sa'=32,'sb'=8] {'sa','sb'}, dimensions={0} | all-to-all | bytes 2097152 | tf_op jit(solution)/shard_map/all_to_all | solution.py:25
  185.7 4.3 stack.2
  190.0 8.4 %all-to-all-start.3 = ((bf16[256,8,2048]{2,1,0:T(8,128)(2,1)}), bf16[256,8,2048]{2,1,0:T(8,128)(2,1)}, u32[]{:S(2)}, u32[]{:S(2)}) async-start(bf16[256,8,2048]{2,1,0:T(8,128)(2,1)} %stack.2), calls=%async_computation.3 | async-start | bytes 16777216 | tf_op jit(solution)/shard_map/all_to_all | solution.py:40
  202.9 183.2 %all-to-all-done.3 = bf16[256,8,2048]{2,1,0:T(8,128)(2,1)} async-done(((bf16[256,8,2048]{2,1,0:T(8,128)(2,1)}), bf16[256,8,2048]{2,1,0:T(8,128)(2,1)}, u32[]{:S(2)}, u32[]{:S(2)}) %all-to-all-start.3) | async-done | bytes 8388640 | tf_op jit(solution)/shard_map/all_to_all | solution.py:40
  386.1 9.3 %fusion.10 = (bf16[2,4,32,2048]{3,2,1,0:T(8,128)(2,1)S(1)}, bf16[2,4,32,2048]{3,2,1,0:T(8,128)(2,1)}, f32[2,4,32,2048]{3,2,1,0:T(8,128)}) fusion(bf16[2,4,32,2048]{3,2,1,0:T(8,128)(2,1)} %param.13, f32[2,4,32,2048]{3,2,1,0:T(8,128)} %convolution_bitcast_fusion, bf16[2,4,32,2048]{3,2,1,0:T(8,128)(2,1)} %param.7, bf16[256,8,2048]{2,1,0:T(8,128)(2,1)} %all-to-all-done.3, ...), kind=kOutput, calls=%fused_computation.16 | convolution fusion | flops 2155347968 | bytes 16786432 | tf_op jit(solution)/shard_map/tr,rc->tc/dot_general | solution.py:31
  397.0 37.4 %all_to_all.65 = bf16[256,8,256]{2,1,0:T(8,128)(2,1)S(1)} all-to-all(bf16[256,8,256]{2,1,0:T(8,128)(2,1)S(1)} %copy.156), channel_id=1, replica_groups=mesh['sa'=32,'sb'=8] {'sa','sb'}, dimensions={0} | all-to-all | bytes 2097152 | tf_op jit(solution)/shard_map/all_to_all | solution.py:15
  434.6 2.3 copy.137
  437.0 2.2 reshape.137
  439.1 2.9 fusion.27
  442.5 2.2 reshape.149
  444.8 5.9 %all-to-all-start.6 = ((bf16[32,2,1024]{2,1,0:T(2,128)(2,1)}), bf16[32,2,1024]{2,1,0:T(2,128)(2,1)}, u32[]{:S(2)}, u32[]{:S(2)}) async-start(bf16[32,2,1024]{2,1,0:T(2,128)(2,1)} %reshape.149), calls=%async_computation.6 | async-start | bytes 262144 | tf_op jit(solution)/shard_map/all_to_all | solution.py:71
  453.7 5.6 %all-to-all-done.6 = bf16[32,2,1024]{2,1,0:T(2,128)(2,1)} async-done(((bf16[32,2,1024]{2,1,0:T(2,128)(2,1)}), bf16[32,2,1024]{2,1,0:T(2,128)(2,1)}, u32[]{:S(2)}, u32[]{:S(2)}) %all-to-all-start.6) | async-done | bytes 131104 | tf_op jit(solution)/shard_map/all_to_all | solution.py:71
  464.9 2.0 reshape.151
  466.9 4.1 all-to-all-start.7
  476.5 6.0 %all-to-all-done.7 = bf16[8,2,12288]{2,1,0:T(2,128)(2,1)} async-done(((bf16[8,2,12288]{2,1,0:T(2,128)(2,1)}), bf16[8,2,12288]{2,1,0:T(2,128)(2,1)}, u32[]{:S(2)}, u32[]{:S(2)}) %all-to-all-start.7) | async-done | bytes 393248 | tf_op jit(solution)/shard_map/all_to_all | solution.py:82
  482.5 10.8 %all-to-all-start.5 = ((bf16[256,8,256]{2,1,0:T(8,128)(2,1)}), bf16[256,8,256]{2,1,0:T(8,128)(2,1)}, u32[]{:S(2)}, u32[]{:S(2)}) async-start(bf16[256,8,256]{2,1,0:T(8,128)(2,1)} %copy.142), calls=%async_computation.5 | async-start | bytes 2097152 | tf_op jit(solution)/shard_map/all_to_all | solution.py:25
  494.4 2.6 reshape.152
  499.5 24.2 %all-to-all-done.5 = bf16[256,8,256]{2,1,0:T(8,128)(2,1)} async-done(((bf16[256,8,256]{2,1,0:T(8,128)(2,1)}), bf16[256,8,256]{2,1,0:T(8,128)(2,1)}, u32[]{:S(2)}, u32[]{:S(2)}) %all-to-all-start.5) | async-done | bytes 1048608 | tf_op jit(solution)/shard_map/all_to_all | solution.py:25
  526.7 8.4 %fusion.21 = (f32[2,4,32]{2,1,0:T(4,128)S(1)}, f32[2,4,32,2048]{3,2,1,0:T(8,128)S(1)}) fusion(bf16[2,4,32,2048]{3,2,1,0:T(8,128)(2,1)S(1)} %copy-done.4, f32[2048]{0:T(1024)S(1)} %copy-done.14, f32[2,4,32,2048]{3,2,1,0:T(8,128)} %reshape.143, bf16[256,8,2048]{2,1,0:T(8,128)(2,1)} %all-to-all-done.3, f32[2,4,32,2048]{3,2,1,0:T(8,128)} %convolution_bitcast_fusion, ...), kind=kOutput, calls=%fused_computation.27 | convolution fusion | flops 2155872000 | bytes 18883584 | tf_op jit(solution)/shard_map/tc,rc->tr/dot_general | solution.py:31
  (78 shorter events, 39.7 us)
Async XLA Ops:
  0.6 200.5 %copy-start = (bf16[2,4,32,32]{3,2,1,0:T(8,128)(2,1)S(1)}, bf16[2,4,32,32]{3,2,1,0:T(8,128)(2,1)}, u32[]{:S(2)}) copy-start(bf16[2,4,32,32]{3,2,1,0:T(8,128)(2,1)} %param.12) | copy-start | bytes 49156
  0.6 57.0 %copy-start.3 = (bf16[2,4,32,2048]{3,2,1,0:T(8,128)(2,1)S(1)}, bf16[2,4,32,2048]{3,2,1,0:T(8,128)(2,1)}, u32[]{:S(2)}) copy-start(bf16[2,4,32,2048]{3,2,1,0:T(8,128)(2,1)} %param.7) | copy-start | bytes 3145732
  0.7 57.3 %copy-start.14 = (f32[2048]{0:T(1024)S(1)}, f32[2048]{0:T(1024)}, u32[]{:S(2)}) copy-start(f32[2048]{0:T(1024)} %param.8) | copy-start | bytes 24580
  44.7 21.4 %all-to-all-start.1 = ((bf16[32,2,1024]{2,1,0:T(2,128)(2,1)}), bf16[32,2,1024]{2,1,0:T(2,128)(2,1)S(1)}, u32[]{:S(2)}, u32[]{:S(2)}) async-start(bf16[32,2,1024]{2,1,0:T(2,128)(2,1)} %reshape.147), calls=%async_computation.1 | async-start | bytes 262144 | tf_op jit(solution)/shard_map/all_to_all | solution.py:44
  58.5 17.5 %copy-start.12 = (bf16[4,1,64,64]{3,2,1,0:T(8,128)(2,1)S(1)}, bf16[4,1,64,64]{3,2,1,0:T(8,128)(2,1)}, u32[]{:S(2)}) copy-start(bf16[4,1,64,64]{3,2,1,0:T(8,128)(2,1)} %param.10) | copy-start | bytes 98308
  66.1 70.3 %all-to-all-start = ((bf16[256,8,256]{2,1,0:T(8,128)(2,1)}), bf16[256,8,256]{2,1,0:T(8,128)(2,1)S(1)}, u32[]{:S(2)}, u32[]{:S(2)}) async-start(bf16[256,8,256]{2,1,0:T(8,128)(2,1)} %copy.154), calls=%async_computation | async-start | bytes 2097152 | tf_op jit(solution)/shard_map/all_to_all | solution.py:15
  136.2 2.0 copy-start.7
  136.4 2.2 copy-start.5
  141.9 43.8 %copy-start.13 = (bf16[8,2048]{1,0:T(8,128)(2,1)S(1)}, bf16[8,2048]{1,0:T(8,128)(2,1)}, u32[]{:S(2)}) copy-start(bf16[8,2048]{1,0:T(8,128)(2,1)} %param.9) | copy-start | bytes 98308
  190.0 196.1 %all-to-all-start.3 = ((bf16[256,8,2048]{2,1,0:T(8,128)(2,1)}), bf16[256,8,2048]{2,1,0:T(8,128)(2,1)}, u32[]{:S(2)}, u32[]{:S(2)}) async-start(bf16[256,8,2048]{2,1,0:T(8,128)(2,1)} %stack.2), calls=%async_computation.3 | async-start | bytes 16777216 | tf_op jit(solution)/shard_map/all_to_all | solution.py:40
  395.4 1.0 copy-start.9
  439.1 2.9 copy-start.2
  439.1 2.9 copy-start.6
  444.8 14.5 %all-to-all-start.6 = ((bf16[32,2,1024]{2,1,0:T(2,128)(2,1)}), bf16[32,2,1024]{2,1,0:T(2,128)(2,1)}, u32[]{:S(2)}, u32[]{:S(2)}) async-start(bf16[32,2,1024]{2,1,0:T(2,128)(2,1)} %reshape.149), calls=%async_computation.6 | async-start | bytes 262144 | tf_op jit(solution)/shard_map/all_to_all | solution.py:71
  460.6 10.4 %copy-start.8 = (bf16[32,1,64,64]{3,2,1,0:T(8,128)(2,1)S(1)}, bf16[32,1,64,64]{3,2,1,0:T(8,128)(2,1)}, u32[]{:S(2)}) copy-start(bf16[32,1,64,64]{3,2,1,0:T(8,128)(2,1)} %copy-done.7) | copy-start | bytes 786436
  466.9 15.6 %all-to-all-start.7 = ((bf16[8,2,12288]{2,1,0:T(2,128)(2,1)}), bf16[8,2,12288]{2,1,0:T(2,128)(2,1)}, u32[]{:S(2)}, u32[]{:S(2)}) async-start(bf16[8,2,12288]{2,1,0:T(2,128)(2,1)} %reshape.151), calls=%async_computation.7 | async-start | bytes 786432 | tf_op jit(solution)/shard_map/all_to_all | solution.py:82
  475.0 18.3 %copy-start.10 = (bf16[2,4,32,2048]{3,2,1,0:T(8,128)(2,1)S(1)}, bf16[2,4,32,2048]{3,2,1,0:T(8,128)(2,1)}, u32[]{:S(2)}) copy-start(bf16[2,4,32,2048]{3,2,1,0:T(8,128)(2,1)} %copy-done.9) | copy-start | bytes 3145732
  482.5 41.2 %all-to-all-start.5 = ((bf16[256,8,256]{2,1,0:T(8,128)(2,1)}), bf16[256,8,256]{2,1,0:T(8,128)(2,1)}, u32[]{:S(2)}, u32[]{:S(2)}) async-start(bf16[256,8,256]{2,1,0:T(8,128)(2,1)} %copy.142), calls=%async_computation.5 | async-start | bytes 2097152 | tf_op jit(solution)/shard_map/all_to_all | solution.py:25
  525.1 1.5 copy-start.4
  526.7 8.5 %copy-start.11 = (bf16[2,4,32,2048]{3,2,1,0:T(8,128)(2,1)S(1)}, bf16[2,4,32,2048]{3,2,1,0:T(8,128)(2,1)}, u32[]{:S(2)}) copy-start(bf16[2,4,32,2048]{3,2,1,0:T(8,128)(2,1)} %param.13) | copy-start | bytes 3145732
  535.1 1.6 copy-start.1
